TPU v7x, 1024 devices: a whole 8x8x8 slice. The times are simulated.
1024 devices in a mesh: grp: 64 (over y, x_lo, core), tile: 16 (over z, x_hi).
Axes of the slice: x: 8 (x_hi: 2, x_lo: 4; x = x_hi * 4 + x_lo), y: 8, z: 8, core: 2. Of those that a mesh axis runs over, the one named last changes fastest.
Arguments:
- atm_flux: float32 [6, 1048576], P(None, ('grp', 'tile')), may hold values from -6 to 6
- send_block: int32 [1024, 16, 4], P(('grp', 'tile')), may hold values from 0 to 7
- send_count: int32 [1024, 16], P(('grp', 'tile')), may hold values from 1 to 4, as said below
- recv_block: int32 [1024, 16, 4], P(('grp', 'tile')), may hold values from 0 to 63
- recv_weight: bfloat16 [1024, 16, 4, 128, 128], P(('grp', 'tile')), may hold values from -0.5 to 0.5
- sea_temp: float32 [2048, 4096], P('grp', 'tile'), may hold values from -6 to 6
- ocean_mask: int32 [2048, 4096], P('grp', 'tile'), may hold values 0 or 1
Outputs:
- heat_flux: float32 [2048, 4096], P('grp', 'tile')
- stress_curl: float32 [2048, 4096], P('grp', 'tile')
- atm_return: float32 [4, 1048576], P(None, ('grp', 'tile'))
Inputs may be any that keep to these rules, and one draw needn't show every extreme that they name: `send_count`: in every draw a quarter of the tile indices, drawn from the seed, receive exactly 4 blocks from every device of their group; every other pair carries 1 to 2 blocks.
All inputs are finite; a program needn't handle non-finite values. No bound on the sum of `ocean_mask` on one device may be relied on, other than what follows from the above.
Results may differ from a plain program's by a relative error of at most 0.0003.
Values sent between devices are 32-bit elements; how exact they have to be, the bound alone decides.
A program may use at most 32 MiB of HBM per device.

v0:
```python
import jax
import jax.numpy as jnp
from jax import lax
from jax.sharding import PartitionSpec as P

precise = lax.Precision.HIGHEST


def extended(value, sides, width):
    edges = {}
    for axis, dim in sides:
        size, length = (lax.axis_size(axis), value.shape[dim])
        up = [(i, (i + 1) % size) for i in range(size)]
        last = lax.slice_in_dim(value, length - width, length, axis=dim)
        initial = lax.slice_in_dim(value, 0, width, axis=dim)
        edges[dim] = (
            lax.ppermute(last, axis, up),
            lax.ppermute(initial, axis, [(b, a) for a, b in up]),
        )
    done = []
    for _, dim in sides:
        low, high = edges[dim]
        around = [(width, width) if d in done else (0, 0) for d in range(value.ndim)]
        value = jnp.concatenate([jnp.pad(low, around), value, jnp.pad(high, around)], axis=dim)
        done.append(dim)
    return value


def from_partner(value, axis, stride):
    return lax.ppermute(value, axis, [(i, i ^ 1 << stride) for i in range(lax.axis_size(axis))])


def bulk_formula(fields, surface_temp, ocean_mask):
    sea_share = ocean_mask.astype(jnp.float32)
    wind_u, wind_v, air_temp, air_vapor, short_down, long_down = [fields[k] for k in range(6)]
    wind_speed = jnp.sqrt(wind_u * wind_u + wind_v * wind_v + 0.5)
    stress_x = 0.8 * wind_speed * wind_u * sea_share
    stress_y = 0.8 * wind_speed * wind_v * sea_share
    sensible = 0.6 * wind_speed * (surface_temp - air_temp)
    latent = 0.7 * wind_speed * (jnp.exp(0.3 * surface_temp) - air_vapor)
    long_up = 0.4 * (1.0 + 0.2 * surface_temp) ** 4
    heat_flux = (0.94 * short_down + long_down - long_up - sensible - latent) * sea_share
    surface = jnp.stack([surface_temp, sensible, latent, long_up]) * sea_share[None]
    return (stress_x, stress_y, heat_flux, surface)


def per_device(atm_flux, send_block, send_count, recv_block, recv_weight, sea_temp, ocean_mask):
    tile_count = lax.axis_size("tile")
    field_count = atm_flux.shape[0]
    block_cells = recv_weight.shape[-1]
    slot_count = send_block.shape[2]
    atm_blocks = atm_flux.shape[1] // block_cells
    ocean_rows, ocean_cols = sea_temp.shape
    ocean_blocks = ocean_rows * ocean_cols // block_cells
    slot_range = jnp.arange(slot_count, dtype=jnp.int32)
    blocks = atm_flux.reshape(field_count, atm_blocks, block_cells)
    send_index = send_block[0]
    pair_count = send_count[0]
    live_slots = (slot_range[None, :] < pair_count[:, None]).astype(jnp.float32)
    chosen = jnp.take(blocks, send_index, axis=1) * live_slots[None, :, :, None]
    incoming = lax.all_to_all(chosen, "tile", split_axis=1, concat_axis=1, tiled=True)
    weight_wide = recv_weight[0].astype(jnp.float32)
    remapped = jnp.einsum("scij,fscj->fsci", weight_wide, incoming, precision=precise)
    dest_block = recv_block[0]
    onehot = (
        jnp.arange(ocean_blocks, dtype=jnp.int32)[:, None] == dest_block.reshape(-1)[None, :]
    ).astype(jnp.float32)
    landed = jnp.einsum(
        "ok,fkj->foj",
        onehot,
        remapped.reshape(field_count, tile_count * slot_count, block_cells),
        precision=precise,
    )
    fields = landed.reshape(field_count, ocean_rows, ocean_cols)
    stress_x, stress_y, heat_flux, surface = bulk_formula(fields, sea_temp, ocean_mask)
    sea_share = ocean_mask.astype(jnp.float32)
    padded = extended(jnp.stack([stress_x, stress_y]), (("grp", 1), ("tile", 2)), 1)
    mirror_row = stress_x[ocean_rows - 1]
    for bit_number in range(tile_count.bit_length() - 1):
        mirror_row = from_partner(mirror_row, "tile", bit_number)
    fold_values = -jnp.flip(mirror_row)
    group_index = lax.axis_index("grp")
    south_rim = jnp.where(group_index == 0, 0.0, padded[0, 0, 1:-1])
    north_rim = jnp.where(group_index == lax.axis_size("grp") - 1, fold_values, padded[0, -1, 1:-1])
    column_x = jnp.concatenate([south_rim[None], stress_x, north_rim[None]], axis=0)
    stress_curl = 0.5 * (padded[1, 1:-1, 2:] - padded[1, 1:-1, :-2]) - 0.5 * (
        column_x[2:] - column_x[:-2]
    )
    stress_curl = stress_curl * sea_share
    surface_blocks = surface.reshape(surface.shape[0], ocean_blocks, block_cells)
    chosen_back = jnp.take(surface_blocks, dest_block, axis=1)
    returned = jnp.einsum("scij,fsci->fscj", weight_wide, chosen_back, precision=precise)
    arrived = lax.all_to_all(returned, "tile", split_axis=1, concat_axis=1, tiled=True)
    arrived = arrived * live_slots[None, :, :, None]
    atm_onehot = (
        jnp.arange(atm_blocks, dtype=jnp.int32)[:, None] == send_index.reshape(-1)[None, :]
    ).astype(jnp.float32)
    atm_part = jnp.einsum(
        "ak,fkj->faj",
        atm_onehot,
        arrived.reshape(surface.shape[0], tile_count * slot_count, block_cells),
        precision=precise,
    )
    return (heat_flux, stress_curl, atm_part.reshape(surface.shape[0], atm_blocks * block_cells))


def solution(mesh):
    placed = (
        P(None, ("grp", "tile")),
        P(("grp", "tile"), None, None),
        P(("grp", "tile"), None),
        P(("grp", "tile"), None, None),
        P(("grp", "tile"), None, None, None, None),
        P("grp", "tile"),
        P("grp", "tile"),
    )
    return jax.shard_map(
        per_device,
        mesh=mesh,
        in_specs=placed,
        out_specs=(P("grp", "tile"), P("grp", "tile"), P(None, ("grp", "tile"))),
        check_vma=False,
    )
```

profile of v0, /device:TPU:18, one launch (start us, length us, event | category | flops | bytes accessed | tf_op | source)
XLA Modules:
  0.0 97.0 jit_solution(3836719629169782131)
XLA Ops:
  0.6 0.8 compare_select_fusion.2
  1.5 0.7 compare_and_fusion.1
  2.2 0.7 fusion.29
  3.2 1.4 %gather_fusion = f32[64,6,128]{2,1,0:T(8,128)S(1)} fusion(f32[6,8,128]{2,0,1:T(8,128)} %bitcast.64, s32[1024]{0:T(1024)S(1)} %pad_clamp_fusion.1), kind=kCustom, calls=%fused_computation | custom fusion | bytes 393472 | tf_op jit(solution)/shard_map/jit(_take)/gather | solution.py:60
  4.5 0.8 fusion.10
  5.4 20.9 %all-to-all-start = ((f32[6,16,4,128]{3,2,0,1:T(4,128)}), f32[6,16,4,128]{3,2,0,1:T(4,128)S(1)}, u32[]{:S(2)}, u32[]{:S(2)}) async-start(f32[6,16,4,128]{3,2,0,1:T(4,128)} %fusion.10), calls=%async_computation | async-start | bytes 393216 | tf_op jit(solution)/shard_map/all_to_all | solution.py:61
  26.3 0.7 compare_select_fusion
  27.0 0.8 copy.31
  27.7 0.8 copy.35
  28.6 0.8 convert_element_type.18
  29.4 0.8 stack.27
  30.3 0.7 compare_and_fusion
  31.2 9.8 %all-to-all-done = f32[6,16,4,128]{3,2,0,1:T(4,128)S(1)} async-done(((f32[6,16,4,128]{3,2,0,1:T(4,128)}), f32[6,16,4,128]{3,2,0,1:T(4,128)S(1)}, u32[]{:S(2)}, u32[]{:S(2)}) %all-to-all-start) | async-done | bytes 196640 | tf_op jit(solution)/shard_map/all_to_all | solution.py:61
  41.0 3.3 %fusion.2 = f32[16,4,6,128]{3,2,1,0:T(8,128)S(1)} fusion(bf16[1,16,4,128,128]{4,3,2,1,0:T(8,128)(2,1)S(1)} %copy-done, f32[6,16,4,128]{3,2,0,1:T(4,128)S(1)} %all-to-all-done), kind=kOutput, calls=%fused_computation.4 | convolution fusion | flops 75497472 | bytes 2490368 | tf_op jit(solution)/shard_map/scij,fscj->fsci/dot_general | solution.py:63
  44.4 0.3 convolution_bitcast_fusion
  44.8 0.7 multiply_bitcast_fusion
  45.4 2.8 %collective-permute-start.4 = (f32[256]{0:T(256)S(1)}, f32[256]{0:T(256)S(1)}, u32[]{:S(2)}, u32[]{:S(2)}) collective-permute-start(f32[256]{0:T(256)S(1)} %bitcast.75), channel_id=1, source_target_pairs={{0,1},{1,0},{2,3},{3,2},{4,5},{5,4},{6,7},{7,6},{8,9},{9,8},{10,11... | collective-permute-start | bytes 3080 | tf_op jit(solution)/shard_map/ppermute | solution.py:30
  48.4 1.9 %collective-permute-start.1 = (f32[2,1,256]{2,1,0:T(1,128)S(1)}, f32[2,1,256]{2,1,0:T(1,128)S(1)}, u32[]{:S(2)}, u32[]{:S(2)}) collective-permute-start(f32[2,1,256]{2,1,0:T(1,128)S(1)} %get-tuple-element.18), channel_id=1, source_target_pairs={{16,0},{32,16},{48,32},{64,48},{80,64},{96,80},{112,96},{128,112},... | collective-permute-start | bytes 6152 | tf_op jit(solution)/shard_map/ppermute | solution.py:18
  50.3 2.4 %collective-permute-start = (f32[2,1,256]{2,1,0:T(1,128)S(1)}, f32[2,1,256]{2,1,0:T(1,128)S(1)}, u32[]{:S(2)}, u32[]{:S(2)}) collective-permute-start(f32[2,1,256]{2,1,0:T(1,128)S(1)} %get-tuple-element.19), channel_id=1, source_target_pairs={{0,16},{16,32},{32,48},{48,64},{64,80},{80,96},{96,112},{112,128},... | collective-permute-start | bytes 6152 | tf_op jit(solution)/shard_map/ppermute | solution.py:17
  52.7 6.7 %collective-permute-start.2 = (f32[2,32,1]{2,1,0:T(8,128)S(1)}, f32[2,32,1]{2,1,0:T(8,128)S(1)}, u32[]{:S(2)}, u32[]{:S(2)}) collective-permute-start(f32[2,32,1]{2,1,0:T(8,128)S(1)} %get-tuple-element.16), channel_id=1, source_target_pairs={{1,0},{2,1},{3,2},{4,3},{5,4},{6,5},{7,6},{8,7},{9,8},{10,9},{11,1... | collective-permute-start | bytes 776 | tf_op jit(solution)/shard_map/ppermute | solution.py:18
  59.4 3.1 %collective-permute-start.3 = (f32[2,32,1]{2,1,0:T(8,128)S(1)}, f32[2,32,1]{2,1,0:T(8,128)S(1)}, u32[]{:S(2)}, u32[]{:S(2)}) collective-permute-start(f32[2,32,1]{2,1,0:T(8,128)S(1)} %get-tuple-element.17), channel_id=1, source_target_pairs={{0,1},{1,2},{2,3},{3,4},{4,5},{5,6},{6,7},{7,8},{8,9},{9,10},{10,1... | collective-permute-start | bytes 776 | tf_op jit(solution)/shard_map/ppermute | solution.py:17
  62.6 2.6 %collective-permute-start.5 = (f32[256]{0:T(256)S(1)}, f32[256]{0:T(256)S(1)}, u32[]{:S(2)}, u32[]{:S(2)}) collective-permute-start(f32[256]{0:T(256)S(1)} %collective-permute-done.4), channel_id=1, source_target_pairs={{0,2},{1,3},{2,0},{3,1},{4,6},{5,7},{6,4},{7,5},{8,10},{9,11},{10,... | collective-permute-start | bytes 3080 | tf_op jit(solution)/shard_map/ppermute | solution.py:30
  65.3 0.7 gather_fusion.1
  66.0 2.1 %collective-permute-done.5 = f32[256]{0:T(256)S(1)} collective-permute-done((f32[256]{0:T(256)S(1)}, f32[256]{0:T(256)S(1)}, u32[]{:S(2)}, u32[]{:S(2)}) %collective-permute-start.5) | collective-permute-done | bytes 1056 | tf_op jit(solution)/shard_map/ppermute | solution.py:30
  68.1 2.9 %collective-permute-start.6 = (f32[256]{0:T(256)S(1)}, f32[256]{0:T(256)S(1)}, u32[]{:S(2)}, u32[]{:S(2)}) collective-permute-start(f32[256]{0:T(256)S(1)} %collective-permute-done.5), channel_id=1, source_target_pairs={{0,4},{1,5},{2,6},{3,7},{4,0},{5,1},{6,2},{7,3},{8,12},{9,13},{10,... | collective-permute-start | bytes 3080 | tf_op jit(solution)/shard_map/ppermute | solution.py:30
  71.0 2.5 %fusion.4 = f32[4,16,4,128]{3,0,2,1:T(4,128)} fusion(bf16[1,16,4,128,128]{4,3,2,1,0:T(8,128)(2,1)S(1)} %copy-done, f32[16,4,4,128]{3,2,1,0:T(4,128)S(1)} %bitcast.71, pred[16,4]{1,0:T(8,128)(4,1)S(1)} %copy.33), kind=kOutput, calls=%fused_computation.7 | convolution fusion | flops 50364416 | bytes 2359360 | tf_op jit(solution)/shard_map/scij,fsci->fscj/dot_general | solution.py:92
  73.4 9.7 %all-to-all-start.1 = ((f32[4,16,4,128]{3,0,2,1:T(4,128)}), f32[4,16,4,128]{3,0,2,1:T(4,128)S(1)}, u32[]{:S(2)}, u32[]{:S(2)}) async-start(f32[4,16,4,128]{3,0,2,1:T(4,128)} %fusion.4), calls=%async_computation.1 | async-start | bytes 262144 | tf_op jit(solution)/shard_map/all_to_all | solution.py:93
  83.1 7.7 %collective-permute-start.7 = (f32[256]{0:T(256)S(1)}, f32[256]{0:T(256)S(1)}, u32[]{:S(2)}, u32[]{:S(2)}) collective-permute-start(f32[256]{0:T(256)S(1)} %collective-permute-done.6), channel_id=1, source_target_pairs={{0,8},{1,9},{2,10},{3,11},{4,12},{5,13},{6,14},{7,15},{8,0},{9,1},... | collective-permute-start | bytes 3080 | tf_op jit(solution)/shard_map/ppermute | solution.py:30
  90.9 1.7 %collective-permute-done.7 = f32[256]{0:T(256)S(1)} collective-permute-done((f32[256]{0:T(256)S(1)}, f32[256]{0:T(256)S(1)}, u32[]{:S(2)}, u32[]{:S(2)}) %collective-permute-start.7) | collective-permute-done | bytes 1056 | tf_op jit(solution)/shard_map/ppermute | solution.py:30
  92.7 0.7 fusion.20
  93.4 2.7 %all-to-all-done.1 = f32[4,16,4,128]{3,0,2,1:T(4,128)S(1)} async-done(((f32[4,16,4,128]{3,0,2,1:T(4,128)}), f32[4,16,4,128]{3,0,2,1:T(4,128)S(1)}, u32[]{:S(2)}, u32[]{:S(2)}) %all-to-all-start.1) | async-done | bytes 131104 | tf_op jit(solution)/shard_map/all_to_all | solution.py:93
  96.4 0.6 copy.50
  (42 shorter events, 1.6 us)
Async XLA Ops:
  0.6 40.4 %copy-start = (bf16[1,16,4,128,128]{4,3,2,1,0:T(8,128)(2,1)S(1)}, bf16[1,16,4,128,128]{4,3,2,1,0:T(8,128)(2,1)}, u32[]{:S(2)}) copy-start(bf16[1,16,4,128,128]{4,3,2,1,0:T(8,128)(2,1)} %param.11) | copy-start | bytes 6291460
  5.3 39.4 %copy-start.1 = (s32[32,256]{1,0:T(8,128)S(1)}, s32[32,256]{1,0:T(8,128)}, u32[]{:S(2)}) copy-start(s32[32,256]{1,0:T(8,128)} %param.13) | copy-start | bytes 98308
  5.4 39.4 %copy-start.2 = (f32[32,256]{1,0:T(8,128)S(1)}, f32[32,256]{1,0:T(8,128)}, u32[]{:S(2)}) copy-start(f32[32,256]{1,0:T(8,128)} %param.12) | copy-start | bytes 98308
  5.4 35.7 %all-to-all-start = ((f32[6,16,4,128]{3,2,0,1:T(4,128)}), f32[6,16,4,128]{3,2,0,1:T(4,128)S(1)}, u32[]{:S(2)}, u32[]{:S(2)}) async-start(f32[6,16,4,128]{3,2,0,1:T(4,128)} %fusion.10), calls=%async_computation | async-start | bytes 393216 | tf_op jit(solution)/shard_map/all_to_all | solution.py:61
  45.4 17.2 %collective-permute-start.4 = (f32[256]{0:T(256)S(1)}, f32[256]{0:T(256)S(1)}, u32[]{:S(2)}, u32[]{:S(2)}) collective-permute-start(f32[256]{0:T(256)S(1)} %bitcast.75), channel_id=1, source_target_pairs={{0,1},{1,0},{2,3},{3,2},{4,5},{5,4},{6,7},{7,6},{8,9},{9,8},{10,11... | collective-permute-start | bytes 3080 | tf_op jit(solution)/shard_map/ppermute | solution.py:30
  48.4 42.5 %collective-permute-start.1 = (f32[2,1,256]{2,1,0:T(1,128)S(1)}, f32[2,1,256]{2,1,0:T(1,128)S(1)}, u32[]{:S(2)}, u32[]{:S(2)}) collective-permute-start(f32[2,1,256]{2,1,0:T(1,128)S(1)} %get-tuple-element.18), channel_id=1, source_target_pairs={{16,0},{32,16},{48,32},{64,48},{80,64},{96,80},{112,96},{128,112},... | collective-permute-start | bytes 6152 | tf_op jit(solution)/shard_map/ppermute | solution.py:18
  50.3 40.6 %collective-permute-start = (f32[2,1,256]{2,1,0:T(1,128)S(1)}, f32[2,1,256]{2,1,0:T(1,128)S(1)}, u32[]{:S(2)}, u32[]{:S(2)}) collective-permute-start(f32[2,1,256]{2,1,0:T(1,128)S(1)} %get-tuple-element.19), channel_id=1, source_target_pairs={{0,16},{16,32},{32,48},{48,64},{64,80},{80,96},{96,112},{112,128},... | collective-permute-start | bytes 6152 | tf_op jit(solution)/shard_map/ppermute | solution.py:17
  52.7 40.0 %collective-permute-start.2 = (f32[2,32,1]{2,1,0:T(8,128)S(1)}, f32[2,32,1]{2,1,0:T(8,128)S(1)}, u32[]{:S(2)}, u32[]{:S(2)}) collective-permute-start(f32[2,32,1]{2,1,0:T(8,128)S(1)} %get-tuple-element.16), channel_id=1, source_target_pairs={{1,0},{2,1},{3,2},{4,3},{5,4},{6,5},{7,6},{8,7},{9,8},{10,9},{11,1... | collective-permute-start | bytes 776 | tf_op jit(solution)/shard_map/ppermute | solution.py:18
  59.4 33.3 %collective-permute-start.3 = (f32[2,32,1]{2,1,0:T(8,128)S(1)}, f32[2,32,1]{2,1,0:T(8,128)S(1)}, u32[]{:S(2)}, u32[]{:S(2)}) collective-permute-start(f32[2,32,1]{2,1,0:T(8,128)S(1)} %get-tuple-element.17), channel_id=1, source_target_pairs={{0,1},{1,2},{2,3},{3,4},{4,5},{5,6},{6,7},{7,8},{8,9},{9,10},{10,1... | collective-permute-start | bytes 776 | tf_op jit(solution)/shard_map/ppermute | solution.py:17
  62.6 5.5 %collective-permute-start.5 = (f32[256]{0:T(256)S(1)}, f32[256]{0:T(256)S(1)}, u32[]{:S(2)}, u32[]{:S(2)}) collective-permute-start(f32[256]{0:T(256)S(1)} %collective-permute-done.4), channel_id=1, source_target_pairs={{0,2},{1,3},{2,0},{3,1},{4,6},{5,7},{6,4},{7,5},{8,10},{9,11},{10,... | collective-permute-start | bytes 3080 | tf_op jit(solution)/shard_map/ppermute | solution.py:30
  68.1 15.0 %collective-permute-start.6 = (f32[256]{0:T(256)S(1)}, f32[256]{0:T(256)S(1)}, u32[]{:S(2)}, u32[]{:S(2)}) collective-permute-start(f32[256]{0:T(256)S(1)} %collective-permute-done.5), channel_id=1, source_target_pairs={{0,4},{1,5},{2,6},{3,7},{4,0},{5,1},{6,2},{7,3},{8,12},{9,13},{10,... | collective-permute-start | bytes 3080 | tf_op jit(solution)/shard_map/ppermute | solution.py:30
  73.4 22.6 %all-to-all-start.1 = ((f32[4,16,4,128]{3,0,2,1:T(4,128)}), f32[4,16,4,128]{3,0,2,1:T(4,128)S(1)}, u32[]{:S(2)}, u32[]{:S(2)}) async-start(f32[4,16,4,128]{3,0,2,1:T(4,128)} %fusion.4), calls=%async_computation.1 | async-start | bytes 262144 | tf_op jit(solution)/shard_map/all_to_all | solution.py:93
  83.1 9.5 %collective-permute-start.7 = (f32[256]{0:T(256)S(1)}, f32[256]{0:T(256)S(1)}, u32[]{:S(2)}, u32[]{:S(2)}) collective-permute-start(f32[256]{0:T(256)S(1)} %collective-permute-done.6), channel_id=1, source_target_pairs={{0,8},{1,9},{2,10},{3,11},{4,12},{5,13},{6,14},{7,15},{8,0},{9,1},... | collective-permute-start | bytes 3080 | tf_op jit(solution)/shard_map/ppermute | solution.py:30
where the time goes:
time: 97.9 us; the launch traced here: 97 us
  starting transfers between devices  60.7 us (62%)
  waiting for transfers between devices  16.3 us (17%)
  other arithmetic  6.97 us (7%)
  matrix products  6.23 us (6%)
  local copies, waits for them, and re-layouts  5.92 us (6%)
    all_to_all x1, starting transfers between devices, per_device(): lax.all_to_all(chosen, 'tile', split_axis=1, concat_axis=1, tiled=True)  20.9 us
    ppermute x4, starting transfers between devices, from_partner(): lax.ppermute(value, axis, [(i, i ^ 1 << stride) for i in range(lax.axis_s...  16 us
    all_to_all x1, waiting for transfers between devices, per_device(): lax.all_to_all(chosen, 'tile', split_axis=1, concat_axis=1, tiled=True)  9.8 us
    all_to_all x1, starting transfers between devices, per_device(): lax.all_to_all(returned, 'tile', split_axis=1, concat_axis=1, tiled=True)  9.66 us
    ppermute x2, starting transfers between devices, extended(): lax.ppermute(initial, axis, [(b, a) for a, b in up])  8.6 us
    ppermute x2, starting transfers between devices, extended(): lax.ppermute(last, axis, up)  5.47 us
    ppermute x4, waiting for transfers between devices, from_partner(): lax.ppermute(value, axis, [(i, i ^ 1 << stride) for i in range(lax.axis_s...  3.79 us
    dot_general x1, matrix products, per_device(): jnp.einsum('scij,fscj->fsci', weight_wide, incoming, precision=precise)  3.33 us
  transfers between devices with their start and end apart: 10, of which 4 were waited for; matrix products, arithmetic and copies ran while one was open for 9% of the time, Pallas kernels for 0%

commit v1 on v0

v1 whole, which is shorter than its diff:
```python
import functools

import jax
import jax.numpy as jnp
from jax import lax
from jax.experimental import pallas as pl
from jax.experimental.pallas import tpu as pltpu
from jax.sharding import PartitionSpec as P

MESH = pl.DeviceIdType.MESH
F32 = jnp.float32
BF16 = jnp.bfloat16
NZ = 8
N_TILE = 16
N_GRP = 64
CAP = 4
NF = 6
NB = 4
LANES = 128
OFFSETS = sorted(
    [(dz, dx) for dz in range(NZ) for dx in range(2)],
    key=lambda o: (min(o[0], NZ - o[0]) + 4 * o[1], o),
)
FAR_FIRST = list(range(N_TILE - 1, 0, -1))


def split(value):
    high = value.astype(BF16).astype(F32)
    return high, value - high


def exchange(
    atm_hbm, sb_ref, sc_ref, rb_ref, w_hbm, temp_hbm, mask_hbm,
    heat_ref, curl_ref, back_ref,
    atm, tiles, w, temp, mask, send, recv, rows, surf, ret_send, ret_recv, sxp, halo_send, halo_recv,
    in_sem, fs_sem, fr_sem, bs_sem, br_sem, hs_sem, hr_sem,
):
    g = lax.axis_index("grp")
    t = lax.axis_index("tile")
    z, half = t // 2, lax.rem(t, 2)

    def to_peer(k):
        dz, dx = OFFSETS[k]
        return lax.rem(z + dz, NZ) * 2 + (1 - half if dx else half)

    def from_peer(k):
        dz, dx = OFFSETS[k]
        return lax.rem(z + NZ - dz, NZ) * 2 + (1 - half if dx else half)

    loads = [
        pltpu.make_async_copy(atm_hbm, atm, in_sem.at[0]),
        pltpu.make_async_copy(w_hbm, w, in_sem.at[1]),
        pltpu.make_async_copy(temp_hbm, temp, in_sem.at[2]),
        pltpu.make_async_copy(mask_hbm, mask, in_sem.at[3]),
    ]
    barrier = pltpu.get_barrier_semaphore()
    north, south = lax.rem(g + 1, N_GRP), lax.rem(g + N_GRP - 1, N_GRP)
    for k in FAR_FIRST:
        pl.semaphore_signal(barrier, 1, device_id=(g, to_peer(k)), device_id_type=MESH)
    for other in (north, south):
        pl.semaphore_signal(barrier, 1, device_id=(other, t), device_id_type=MESH)
    for load in loads:
        load.start()

    lane = lax.broadcasted_iota(jnp.int32, (8, LANES), 1)
    dest = jnp.full((8, LANES), -1, jnp.int32)
    for k in range(N_TILE):
        s = from_peer(k)
        for c in range(CAP):
            slot = k * CAP + c
            dest = jnp.where(lax.rem(lane, 64) == slot, rb_ref[c, s], dest)
    row64 = lax.broadcasted_iota(jnp.int32, (64, LANES), 0)
    block_of_row = 2 * lax.rem(row64, 32) + row64 // 32
    dest64 = jnp.concatenate([dest] * 8, axis=0)
    land = jnp.where(block_of_row == dest64, 1.0, 0.0).astype(BF16)
    picks = []
    for part in range(2):
        pick = jnp.full((8, LANES), -1, jnp.int32)
        for k in range(8 * part, 8 * part + 8):
            u = to_peer(k)
            count = jnp.full((8, LANES), sc_ref[0, u], jnp.int32)
            for c in range(CAP):
                mine = (lane // NB == (k - 8 * part) * CAP + c) & (count > c)
                pick = jnp.where(mine, sb_ref[c, u], pick)
        row32 = lax.broadcasted_iota(jnp.int32, (32, LANES), 0)
        lane32 = lax.broadcasted_iota(jnp.int32, (32, LANES), 1)
        pick32 = jnp.concatenate([pick] * 4, axis=0)
        hit = (row32 // NB == pick32) & (lax.rem(row32, NB) == lax.rem(lane32, NB))
        picks.append(jnp.where(hit, 1.0, 0.0).astype(BF16))
    gather_back = jnp.concatenate(picks, axis=1)

    surf[...] = jnp.zeros_like(surf)
    loads[0].wait()
    for b in range(8):
        tiles[b] = atm[:, b * LANES:(b + 1) * LANES]
    for k in range(N_TILE):
        u = to_peer(k)
        count = jnp.full((NF, LANES), sc_ref[0, u], jnp.int32)
        for c in range(CAP):
            send[k, c * NF:(c + 1) * NF, :] = jnp.where(count > c, tiles[sb_ref[c, u]], 0.0)

    pl.semaphore_wait(barrier, N_TILE + 1)
    forward = {}
    for k in FAR_FIRST:
        forward[k] = pltpu.make_async_remote_copy(
            src_ref=send.at[k], dst_ref=recv.at[k], send_sem=fs_sem.at[k], recv_sem=fr_sem.at[k],
            device_id=(g, to_peer(k)), device_id_type=MESH,
        )
        forward[k].start()
    for load in loads[1:]:
        load.wait()

    zeros2 = jnp.zeros((2, LANES), F32)
    for k in range(N_TILE):
        s = from_peer(k)
        if k:
            forward[k].wait_recv()
        source = recv if k else send
        for c in range(CAP):
            value = source[k, c * NF:(c + 1) * NF, :]
            high, low = split(value)
            lhs = jnp.concatenate([high, zeros2, low, zeros2], axis=0).astype(BF16)
            out = lax.dot_general(lhs, w[s, c], (((1,), (1,)), ((), ())), preferred_element_type=F32)
            at = (k * CAP + c) * 8
            rows[at:at + 8, :] = out[:8] + out[8:]

    def landed(f):
        high, low = split(rows[pl.ds(f, 64, stride=8), :])
        rhs = jnp.concatenate([high, low], axis=0).astype(BF16)
        return jnp.dot(land, rhs, preferred_element_type=F32)

    wind_u, wind_v, air_temp, air_vapor, short_down, long_down = [landed(f) for f in range(NF)]
    sea = jnp.concatenate([temp[:, :LANES], temp[:, LANES:]], axis=0)
    share = jnp.concatenate([mask[:, :LANES], mask[:, LANES:]], axis=0).astype(F32)
    speed = jnp.sqrt(wind_u * wind_u + wind_v * wind_v + 0.5)
    sensible = 0.6 * speed * (sea - air_temp)
    latent = 0.7 * speed * (jnp.exp(0.3 * sea) - air_vapor)
    base = 1.0 + 0.2 * sea
    long_up = 0.4 * ((base * base) * (base * base))
    for f, value in enumerate((sea, sensible, latent, long_up)):
        value = value * share
        for h in range(2):
            surf[pl.ds(h, 32, stride=2), f, :] = value[32 * h:32 * h + 32]

    stress_x = 0.8 * speed * wind_u * share
    stress_y = 0.8 * speed * wind_v * share
    heat_ref[...] = (0.94 * short_down + long_down - long_up - sensible - latent) * share

    back = {}

    def start_back(k):
        if k:
            back[k] = pltpu.make_async_remote_copy(
                src_ref=ret_send.at[k], dst_ref=ret_recv.at[k], send_sem=bs_sem.at[k], recv_sem=br_sem.at[k],
                device_id=(g, from_peer(k)), device_id_type=MESH,
            )
            back[k].start()

    order = FAR_FIRST + [0]
    for i, k in enumerate(order):
        s = from_peer(k)
        for c in range(CAP):
            high, low = split(surf[rb_ref[c, s]])
            lhs = jnp.concatenate([high, low], axis=0).astype(BF16)
            out = jnp.dot(lhs, w[s, c], preferred_element_type=F32)
            total = out[:8] + out[8:]
            if k:
                ret_send[k, c * NB:(c + 1) * NB, :] = total[:NB]
            else:
                ret_recv[0, c * NB:(c + 1) * NB, :] = total[:NB]
        if i:
            start_back(order[i - 1])

    left_y, right_y = stress_y[:32], stress_y[32:]
    to_east = jnp.zeros((8, LANES), F32)
    to_west = jnp.zeros((8, LANES), F32)
    for a in range(4):
        east = pltpu.roll(right_y[8 * a:8 * a + 8], a + 1, 1)
        west = left_y[8 * a:8 * a + 8]
        if a:
            west = pltpu.roll(west, a, 1)
        to_east = jnp.where(lane == a, east, to_east)
        to_west = jnp.where(lane == a, west, to_west)
    sxp[0, 8:40, :] = stress_x[:32]
    sxp[1, 8:40, :] = stress_x[32:]
    zeros6 = jnp.zeros((6, LANES), F32)
    top = jnp.concatenate([stress_x[31:32], stress_x[63:64], zeros6], axis=0)
    bottom = jnp.concatenate([stress_x[0:1], stress_x[32:33], zeros6], axis=0)
    halo_send[0] = top
    halo_send[1] = bottom
    halo_send[2] = to_east
    halo_send[3] = to_west
    start_back(0)
    t_next, t_last = lax.rem(t + 1, N_TILE), lax.rem(t + N_TILE - 1, N_TILE)
    targets = ((0, north, t), (1, south, t), (2, g, t_next), (3, g, t_last), (0, g, N_TILE - 1 - t))
    halos = []
    for i, (source, gg, tt) in enumerate(targets):
        copy = pltpu.make_async_remote_copy(
            src_ref=halo_send.at[source], dst_ref=halo_recv.at[i], send_sem=hs_sem.at[i], recv_sem=hr_sem.at[i],
            device_id=(gg, tt), device_id_type=MESH,
        )
        copy.start()
        halos.append(copy)
    for copy in halos:
        copy.wait_recv()

    fold = halo_recv[4]
    first = fold.astype(BF16)
    second = (fold - first.astype(F32)).astype(BF16)
    third = (fold - first.astype(F32) - second.astype(F32)).astype(BF16)
    ri = lax.broadcasted_iota(jnp.int32, (LANES, LANES), 0)
    ci = lax.broadcasted_iota(jnp.int32, (LANES, LANES), 1)
    mirror = jnp.where(ri + ci == LANES - 1, 1.0, 0.0).astype(BF16)
    flipped = (
        jnp.dot(first, mirror, preferred_element_type=F32)
        + jnp.dot(second, mirror, preferred_element_type=F32)
        + jnp.dot(third, mirror, preferred_element_type=F32)
    )
    for h in range(2):
        low_rim = halo_recv[0, h:h + 1, :]
        high_rim = halo_recv[1, h:h + 1, :]
        sxp[h, 7:8, :] = jnp.where(g == 0, 0.0, low_rim)
        sxp[h, 40:41, :] = jnp.where(g == N_GRP - 1, -flipped[1 - h:2 - h, :], high_rim)
    west_pack, east_pack = halo_recv[2], halo_recv[3]
    lane32 = lax.broadcasted_iota(jnp.int32, (32, LANES), 1)
    west_rim = jnp.concatenate(
        [west_pack] + [pltpu.roll(west_pack, LANES - a, 1) for a in range(1, 4)], axis=0
    )
    east_rim = jnp.concatenate([pltpu.roll(east_pack, LANES - 1 - a, 1) for a in range(4)], axis=0)
    left_up, right_up = pltpu.roll(left_y, 1, 1), pltpu.roll(right_y, 1, 1)
    left_dn, right_dn = pltpu.roll(left_y, LANES - 1, 1), pltpu.roll(right_y, LANES - 1, 1)
    edge_w, edge_e = lane32 == 0, lane32 == LANES - 1
    diffs = (
        jnp.where(edge_e, right_dn, left_dn) - jnp.where(edge_w, west_rim, left_up),
        jnp.where(edge_e, east_rim, right_dn) - jnp.where(edge_w, left_up, right_up),
    )
    for h in range(2):
        column = sxp[h, 9:41, :] - sxp[h, 7:39, :]
        curl_ref[32 * h:32 * h + 32, :] = (0.5 * diffs[h] - 0.5 * column) * share[32 * h:32 * h + 32]

    for k in range(1, N_TILE):
        back[k].wait_recv()
    arrived = ret_recv[...].reshape(N_TILE * CAP * NB, LANES)
    high, low = split(arrived)
    back_ref[...] = jnp.dot(gather_back, high.astype(BF16), preferred_element_type=F32) + jnp.dot(
        gather_back, low.astype(BF16), preferred_element_type=F32
    )
    for k in FAR_FIRST:
        forward[k].wait_send()
        back[k].wait_send()
    for copy in halos:
        copy.wait_send()


def write_out(heat_ref, curl_ref, back_ref, heat_out, curl_out, atm_out):
    for h in range(2):
        heat_out[:, h * LANES:(h + 1) * LANES] = heat_ref[32 * h:32 * h + 32, :]
        curl_out[:, h * LANES:(h + 1) * LANES] = curl_ref[32 * h:32 * h + 32, :]
    for b in range(8):
        atm_out[:, b * LANES:(b + 1) * LANES] = back_ref[b * NB:(b + 1) * NB, :]


def per_device(atm_flux, send_block, send_count, recv_block, recv_weight, sea_temp, ocean_mask):
    hbm = pl.BlockSpec(memory_space=pl.ANY)
    smem = pl.BlockSpec(memory_space=pltpu.SMEM)
    vmem = pl.BlockSpec(memory_space=pltpu.VMEM)
    dma = pltpu.SemaphoreType.DMA
    heat, curl, back = pl.pallas_call(
        exchange,
        out_shape=(
            jax.ShapeDtypeStruct((64, LANES), F32),
            jax.ShapeDtypeStruct((64, LANES), F32),
            jax.ShapeDtypeStruct((32, LANES), F32),
        ),
        in_specs=[hbm, smem, smem, smem, hbm, hbm, hbm],
        out_specs=(vmem, vmem, vmem),
        scratch_shapes=[
            pltpu.VMEM((NF, 1024), F32),
            pltpu.VMEM((8, NF, LANES), F32),
            pltpu.VMEM((N_TILE, CAP, LANES, LANES), BF16),
            pltpu.VMEM((32, 256), F32),
            pltpu.VMEM((32, 256), jnp.int32),
            pltpu.VMEM((N_TILE, CAP * NF, LANES), F32),
            pltpu.VMEM((N_TILE, CAP * NF, LANES), F32),
            pltpu.VMEM((512, LANES), F32),
            pltpu.VMEM((64, 8, LANES), F32),
            pltpu.VMEM((N_TILE, CAP * NB, LANES), F32),
            pltpu.VMEM((N_TILE, CAP * NB, LANES), F32),
            pltpu.VMEM((2, 48, LANES), F32),
            pltpu.VMEM((4, 8, LANES), F32),
            pltpu.VMEM((5, 8, LANES), F32),
            dma((4,)),
            dma((N_TILE,)),
            dma((N_TILE,)),
            dma((N_TILE,)),
            dma((N_TILE,)),
            dma((5,)),
            dma((5,)),
        ],
        compiler_params=pltpu.CompilerParams(collective_id=0, has_side_effects=True),
        name="exchange",
    )(
        atm_flux,
        jnp.transpose(send_block[0], (1, 0)),
        send_count,
        jnp.transpose(recv_block[0], (1, 0)),
        recv_weight[0],
        sea_temp,
        ocean_mask,
    )
    return pl.pallas_call(
        write_out,
        out_shape=(
            jax.ShapeDtypeStruct((32, 256), F32),
            jax.ShapeDtypeStruct((32, 256), F32),
            jax.ShapeDtypeStruct((NB, 1024), F32),
        ),
        in_specs=[vmem, vmem, vmem],
        out_specs=(vmem, vmem, vmem),
        name="write_out",
    )(heat, curl, back)


def solution(mesh):
    placed = (
        P(None, ("grp", "tile")),
        P(("grp", "tile"), None, None),
        P(("grp", "tile"), None),
        P(("grp", "tile"), None, None),
        P(("grp", "tile"), None, None, None, None),
        P("grp", "tile"),
        P("grp", "tile"),
    )
    return jax.shard_map(
        per_device,
        mesh=mesh,
        in_specs=placed,
        out_specs=(P("grp", "tile"), P("grp", "tile"), P(None, ("grp", "tile"))),
        check_vma=False,
    )
```

time: 97.9 us -> 43.1 us (0.44)
  the two profiles are of different devices: /device:TPU:18 before, /device:TPU:1 now
where the time goes in v1:
time: 43.1 us; the launch traced here: 42.3 us
  Pallas kernels  41.7 us (97%)
  between operations  0.64 us (1%)
    pallas_call x1, Pallas kernels, per_device(): pl.pallas_call(exchange, out_shape=(jax.ShapeDtypeStruct((64, LANES), F32...  40.3 us
    pallas_call x1, Pallas kernels, per_device(): pl.pallas_call(write_out, out_shape=(jax.ShapeDtypeStruct((32, 256), F32)...  1.41 us

profile of v1, /device:TPU:1, one launch (start us, length us, event | category | flops | bytes accessed | tf_op | source)
XLA Modules:
  0.0 42.3 jit_solution(4407781679687708701)
XLA Ops:
  0.6 40.3 %exchange.1 = (f32[64,128]{1,0:T(8,128)}, f32[64,128]{1,0:T(8,128)}, f32[32,128]{1,0:T(8,128)}) custom-call(f32[6,1024]{1,0:T(8,128)} %atm_hbm.1, s32[4,16]{1,0:T(4,128)} %bitcast.8, s32[1,16]{1,0:T(1,128)} %sc_ref.1, s32[4,16]{1,0:T(4,128)} %bitcast.9, bf16[16,4,128,128]{3,2,1,0:T(8,128)(2,1)} %bitcast.7, f32[32,256]{1,0:T(8,128)} %temp_hbm.1, ...), custom_call_target="tpu_custom_call" | custom-call | tf_op jit(solution)/shard_map/exchange/pallas_call | solution.py:268
  40.9 1.4 %write_out.1 = (f32[32,256]{1,0:T(8,128)}, f32[32,256]{1,0:T(8,128)}, f32[4,1024]{1,0:T(4,128)}) custom-call(f32[64,128]{1,0:T(8,128)} %get-tuple-element.6.heat_ref, f32[64,128]{1,0:T(8,128)} %get-tuple-element.7.curl_ref, f32[32,128]{1,0:T(8,128)} %get-tuple-element.8.back_ref), custom_call_target="tpu_custom_call" | custom-call | tf_op jit(solution)/shard_map/write_out/pallas_call | solution.py:311

commit v2 on v1

v2 whole, which is shorter than its diff:
```python
import functools

import jax
import jax.numpy as jnp
from jax import lax
from jax.experimental import pallas as pl
from jax.experimental.pallas import tpu as pltpu
from jax.sharding import PartitionSpec as P

MESH = pl.DeviceIdType.MESH
F32 = jnp.float32
BF16 = jnp.bfloat16
NZ = 8
N_TILE = 16
N_GRP = 64
CAP = 4
NF = 6
NB = 4
LANES = 128
N_PEER = 16
HALF = CAP * NF


def split(value):
    high = value.astype(BF16).astype(F32)
    return high, value - high


def exchange(
    atm_hbm, sb_hbm, sc_hbm, rb_hbm, w_hbm, temp_hbm, mask_hbm,
    heat_ref, curl_ref, back_ref,
    atm, sb_ref, sc_ref, rb_ref, tiles, w, temp, mask, send, recv, cross, pass_up, pass_over, rows, surf, ret_send, ret_recv,
    sxp, halo_send, halo_recv,
    in_sem, fs_sem, fr_sem, cs_sem, xr_sem, us_sem, ur_sem, os_sem, or_sem, bs_sem, br_sem, hs_sem, hr_sem,
    column_in, partner_in, group_in,
):
    g = lax.axis_index("grp")
    t = lax.axis_index("tile")
    half = lax.rem(t, 2)
    partner = t + 1 - 2 * half
    shift = 1 - jnp.minimum(g, 1)
    z = lax.rem(t // 2 + (NZ - 1) * shift, NZ)

    def at_level(j, column):
        return lax.rem(j + shift, NZ) * 2 + column

    def peer(k):
        return at_level(k, half) if k < NZ else at_level(k - NZ, 1 - half)

    loads = [
        pltpu.make_async_copy(atm_hbm, atm, in_sem.at[0]),
        pltpu.make_async_copy(sb_hbm, sb_ref, in_sem.at[1]),
        pltpu.make_async_copy(sc_hbm, sc_ref, in_sem.at[2]),
        pltpu.make_async_copy(rb_hbm, rb_ref, in_sem.at[3]),
        pltpu.make_async_copy(w_hbm, w, in_sem.at[4]),
        pltpu.make_async_copy(temp_hbm, temp, in_sem.at[5]),
        pltpu.make_async_copy(mask_hbm, mask, in_sem.at[6]),
    ]
    for load in loads[:4]:
        load.start()
    up, down = g < N_GRP - 1, g > 0
    last8, first8 = lax.rem(g, 8) == 7, lax.rem(g, 8) == 0
    barrier = pltpu.get_barrier_semaphore()
    for j in range(NZ - 1, 0, -1):
        @pl.when(z < j)
        def _():
            pl.semaphore_signal(barrier, 1, device_id=(g, peer(j)), device_id_type=MESH)

    @pl.when(up & jnp.logical_not(last8))
    def _():
        pl.semaphore_signal(barrier, 1, device_id=(g + 1, t), device_id_type=MESH)

    @pl.when(down & first8)
    def _():
        pl.semaphore_signal(barrier, 1, device_id=(g - 1, t), device_id_type=MESH)

    for load in loads[4:]:
        load.start()
    is_last8, not_first8 = lax.rem(g, 8) // 7, jnp.minimum(lax.rem(g, 8), 1)
    below = jnp.minimum(g, 1) * not_first8
    above = is_last8 * jnp.minimum(N_GRP - 1 - g, 1)
    earlier = z + half + below + above
    pl.when(earlier > 0)(lambda: pl.semaphore_wait(barrier, earlier))

    @pl.when(half == 0)
    def _():
        pl.semaphore_signal(barrier, 1, device_id=(g, partner), device_id_type=MESH)

    @pl.when(half == 1)
    def _():
        pl.semaphore_signal(partner_in, 1, device_id=(g, partner), device_id_type=MESH)

    for j in (3, 2, 4, 1, 5, 0, 6):
        @pl.when(z > j)
        def _():
            pl.semaphore_signal(column_in.at[z], 1, device_id=(g, peer(j)), device_id_type=MESH)

    @pl.when(up & last8)
    def _():
        pl.semaphore_signal(group_in.at[0], 1, device_id=(g + 1, t), device_id_type=MESH)

    @pl.when(down & jnp.logical_not(first8))
    def _():
        pl.semaphore_signal(group_in.at[1], 1, device_id=(g - 1, t), device_id_type=MESH)

    for load in loads[:4]:
        load.wait()
    for b in range(8):
        tiles[b] = atm[:, b * LANES:(b + 1) * LANES]
    for k in range(N_PEER):
        u = peer(k)
        count = jnp.full((NF, LANES), sc_ref[0, u], jnp.int32)
        for c in range(CAP):
            at = (k // NZ) * HALF + c * NF
            send[k % NZ, at:at + NF, :] = jnp.where(count > c, tiles[sb_ref[c, u]], 0.0)
    own, other = pl.ds(0, HALF), pl.ds(HALF, HALF)
    recv[z] = send[z, own]

    def copy_to(source, target, send_sem, recv_sem, tt):
        return pltpu.make_async_remote_copy(
            src_ref=source, dst_ref=target, send_sem=send_sem, recv_sem=recv_sem,
            device_id=(g, tt), device_id_type=MESH,
        )

    def own_copy(j):
        return copy_to(send.at[j, own], recv.at[z], fs_sem.at[j], fr_sem.at[z], peer(j))

    def own_in(j):
        return copy_to(send.at[j, own], recv.at[j], fs_sem.at[j], fr_sem.at[j], peer(j))

    def other_over(j):
        return copy_to(send.at[j, other], pass_over.at[z], cs_sem.at[j], or_sem.at[z], peer(j))

    def over_in(j):
        return copy_to(send.at[j, other], pass_over.at[j], cs_sem.at[j], or_sem.at[j], peer(j))

    def other_direct(j):
        return copy_to(send.at[j, other], cross.at[z], cs_sem.at[j], xr_sem.at[z], at_level(j, 1 - half))

    def other_up(j):
        return copy_to(send.at[j, other], pass_up.at[j], cs_sem.at[j], ur_sem.at[j], partner)

    def forward_up(j):
        return copy_to(pass_up.at[j], cross.at[z], us_sem.at[j], xr_sem.at[z], peer(j))

    def forward_over(j):
        return copy_to(pass_over.at[j], cross.at[j], os_sem.at[j], xr_sem.at[j], partner)

    for j in (3, 2, 4, 1, 5, 0, 6):
        @pl.when(z > j)
        def _():
            @pl.when(half == 0)
            def _():
                other_over(j).start()

            @pl.when(half == 1)
            def _():
                other_direct(j).start()

            own_copy(j).start()

    @pl.when(half == 0)
    def _():
        pl.semaphore_wait(partner_in, 1)

    other_direct(z).start()
    for j in range(1, NZ):
        @pl.when(z < j)
        def _():
            other_up(j).start()
    for j in range(1, NZ):
        @pl.when(z < j)
        def _():
            pl.semaphore_wait(column_in.at[j], 1)
            own_copy(j).start()
    def pass_on_up():
        for j in range(1, NZ):
            @pl.when(z < j)
            def _():
                other_up(j).wait_recv()
                forward_up(j).start()

    pl.when(z < NZ // 2)(pass_on_up)
    for j in range(1, NZ):
        @pl.when((z < j) & (half == 0))
        def _():
            over_in(j).wait_recv()
            forward_over(j).start()
    pl.when(z >= NZ // 2)(pass_on_up)

    lane = lax.broadcasted_iota(jnp.int32, (8, LANES), 1)
    dest = jnp.full((8, LANES), -1, jnp.int32)
    for k in range(N_PEER):
        for c in range(CAP):
            dest = jnp.where(lax.rem(lane, 64) == k * CAP + c, rb_ref[c, peer(k)], dest)
    row64 = lax.broadcasted_iota(jnp.int32, (64, LANES), 0)
    block_of_row = 2 * lax.rem(row64, 32) + row64 // 32
    land = jnp.where(block_of_row == jnp.concatenate([dest] * 8, axis=0), 1.0, 0.0).astype(BF16)

    for load in loads[4:]:
        load.wait()
    zeros2 = jnp.zeros((2, LANES), F32)

    def products(k):
        source = recv.at[k] if k < NZ else cross.at[k - NZ]
        for c in range(CAP):
            high, low = split(source[c * NF:(c + 1) * NF, :])
            lhs = jnp.concatenate([high, zeros2, low, zeros2], axis=0).astype(BF16)
            out = lax.dot_general(lhs, w[peer(k), c], (((1,), (1,)), ((), ())), preferred_element_type=F32)
            at = (k * CAP + c) * 8
            rows[at:at + 8, :] = out[:8] + out[8:]

    def cross_in(j):
        return copy_to(send.at[j, other], cross.at[j], cs_sem.at[j], xr_sem.at[j], partner)

    for first in (0, 4):
        for j in range(first, first + 4):
            @pl.when(z != j)
            def _():
                own_in(j).wait_recv()
        for j in range(first, first + 4):
            products(j)
    for first in (0, 4):
        for j in range(first, first + 4):
            cross_in(j).wait_recv()
        for j in range(first, first + 4):
            products(NZ + j)

    def landed(f):
        high, low = split(rows[pl.ds(f, 64, stride=8), :])
        rhs = jnp.concatenate([high, low], axis=0).astype(BF16)
        return jnp.dot(land, rhs, preferred_element_type=F32)

    surf[...] = jnp.zeros_like(surf)
    wind_u, wind_v, air_temp, air_vapor, short_down, long_down = [landed(f) for f in range(NF)]
    sea = jnp.concatenate([temp[:, :LANES], temp[:, LANES:]], axis=0)
    share = jnp.concatenate([mask[:, :LANES], mask[:, LANES:]], axis=0).astype(F32)
    speed = jnp.sqrt(wind_u * wind_u + wind_v * wind_v + 0.5)
    sensible = 0.6 * speed * (sea - air_temp)
    latent = 0.7 * speed * (jnp.exp(0.3 * sea) - air_vapor)
    base = 1.0 + 0.2 * sea
    long_up = 0.4 * ((base * base) * (base * base))
    for f, value in enumerate((sea, sensible, latent, long_up)):
        value = value * share
        for h in range(2):
            surf[pl.ds(h, 32, stride=2), f, :] = value[32 * h:32 * h + 32]

    stress_x = 0.8 * speed * wind_u * share
    stress_y = 0.8 * speed * wind_v * share
    heat_ref[...] = (0.94 * short_down + long_down - long_up - sensible - latent) * share

    left_y, right_y = stress_y[:32], stress_y[32:]
    to_east = jnp.zeros((8, LANES), F32)
    to_west = jnp.zeros((8, LANES), F32)
    for a in range(4):
        east = pltpu.roll(right_y[8 * a:8 * a + 8], a + 1, 1)
        west = left_y[8 * a:8 * a + 8]
        if a:
            west = pltpu.roll(west, a, 1)
        to_east = jnp.where(lane == a, east, to_east)
        to_west = jnp.where(lane == a, west, to_west)
    sxp[0, 8:40, :] = stress_x[:32]
    sxp[1, 8:40, :] = stress_x[32:]
    zeros6 = jnp.zeros((6, LANES), F32)
    halo_send[0] = jnp.concatenate([stress_x[31:32], stress_x[63:64], zeros6], axis=0)
    halo_send[1] = jnp.concatenate([stress_x[0:1], stress_x[32:33], zeros6], axis=0)
    halo_send[2] = to_east
    halo_send[3] = to_west
    def halo(i, source, gg, tt):
        return pltpu.make_async_remote_copy(
            src_ref=halo_send.at[source], dst_ref=halo_recv.at[i], send_sem=hs_sem.at[i], recv_sem=hr_sem.at[i],
            device_id=(gg, tt), device_id_type=MESH,
        )

    t_next, t_last = lax.rem(t + 1, N_TILE), lax.rem(t + N_TILE - 1, N_TILE)
    to_north, to_south = halo(0, 0, g + 1, t), halo(1, 1, g - 1, t)
    around = [halo(2, 2, g, t_next), halo(3, 3, g, t_last)]
    across = halo(4, 0, g, N_TILE - 1 - t)
    def send_halos():
        for copy in around:
            copy.start()
        pl.when(down & first8)(lambda: pl.semaphore_wait(group_in.at[0], 1))
        pl.when(up & jnp.logical_not(last8))(lambda: pl.semaphore_wait(group_in.at[1], 1))
        pl.when(down)(lambda: to_south.start())
        pl.when(up)(lambda: to_north.start())
        pl.when(g == N_GRP - 1)(lambda: across.start())

    def back(k):
        mine = z if k < NZ else NZ + z
        return pltpu.make_async_remote_copy(
            src_ref=ret_send.at[k], dst_ref=ret_recv.at[mine], send_sem=bs_sem.at[k], recv_sem=br_sem.at[mine],
            device_id=(g, peer(k)), device_id_type=MESH,
        )

    def back_in(k):
        return pltpu.make_async_remote_copy(
            src_ref=ret_send.at[k], dst_ref=ret_recv.at[k], send_sem=bs_sem.at[k], recv_sem=br_sem.at[k],
            device_id=(g, peer(k)), device_id_type=MESH,
        )

    def if_other(k, act):
        if k < NZ:
            pl.when(z != k)(act)
        else:
            act()

    order = [k for j in range(NZ) for k in (NZ + j, j)]
    for i, k in enumerate(order):
        for c in range(CAP):
            high, low = split(surf[rb_ref[c, peer(k)]])
            lhs = jnp.concatenate([high, low], axis=0).astype(BF16)
            out = jnp.dot(lhs, w[peer(k), c], preferred_element_type=F32)
            ret_send[k, c * NB:(c + 1) * NB, :] = out[:NB] + out[8:8 + NB]
        if i:
            if_other(order[i - 1], lambda: back(order[i - 1]).start())
        if i == 3:
            send_halos()

    if_other(order[-1], lambda: back(order[-1]).start())
    ret_recv[z] = ret_send[z]

    picks = []
    row32 = lax.broadcasted_iota(jnp.int32, (32, LANES), 0)
    lane32 = lax.broadcasted_iota(jnp.int32, (32, LANES), 1)
    for part in range(2):
        pick = jnp.full((8, LANES), -1, jnp.int32)
        for k in range(8 * part, 8 * part + 8):
            count = jnp.full((8, LANES), sc_ref[0, peer(k)], jnp.int32)
            for c in range(CAP):
                chosen = (lane // NB == (k - 8 * part) * CAP + c) & (count > c)
                pick = jnp.where(chosen, sb_ref[c, peer(k)], pick)
        pick32 = jnp.concatenate([pick] * 4, axis=0)
        hit = (row32 // NB == pick32) & (lax.rem(row32, NB) == lax.rem(lane32, NB))
        picks.append(jnp.where(hit, 1.0, 0.0).astype(BF16))
    gather_back = jnp.concatenate(picks, axis=1)

    pl.when(up)(lambda: to_south.wait_recv())
    pl.when(down)(lambda: to_north.wait_recv())
    for copy in around:
        copy.wait_recv()
    pl.when(g == N_GRP - 1)(lambda: across.wait_recv())

    fold = halo_recv[4]
    first = fold.astype(BF16)
    second = (fold - first.astype(F32)).astype(BF16)
    third = (fold - first.astype(F32) - second.astype(F32)).astype(BF16)
    ri = lax.broadcasted_iota(jnp.int32, (LANES, LANES), 0)
    ci = lax.broadcasted_iota(jnp.int32, (LANES, LANES), 1)
    mirror = jnp.where(ri + ci == LANES - 1, 1.0, 0.0).astype(BF16)
    flipped = (
        jnp.dot(first, mirror, preferred_element_type=F32)
        + jnp.dot(second, mirror, preferred_element_type=F32)
        + jnp.dot(third, mirror, preferred_element_type=F32)
    )
    for h in range(2):
        sxp[h, 7:8, :] = jnp.where(g == 0, 0.0, halo_recv[0, h:h + 1, :])
        sxp[h, 40:41, :] = jnp.where(g == N_GRP - 1, -flipped[1 - h:2 - h, :], halo_recv[1, h:h + 1, :])
    west_pack, east_pack = halo_recv[2], halo_recv[3]
    west_rim = jnp.concatenate(
        [west_pack] + [pltpu.roll(west_pack, LANES - a, 1) for a in range(1, 4)], axis=0
    )
    east_rim = jnp.concatenate([pltpu.roll(east_pack, LANES - 1 - a, 1) for a in range(4)], axis=0)
    left_up, right_up = pltpu.roll(left_y, 1, 1), pltpu.roll(right_y, 1, 1)
    left_dn, right_dn = pltpu.roll(left_y, LANES - 1, 1), pltpu.roll(right_y, LANES - 1, 1)
    edge_w, edge_e = lane32 == 0, lane32 == LANES - 1
    diffs = (
        jnp.where(edge_e, right_dn, left_dn) - jnp.where(edge_w, west_rim, left_up),
        jnp.where(edge_e, east_rim, right_dn) - jnp.where(edge_w, left_up, right_up),
    )
    for h in range(2):
        column = sxp[h, 9:41, :] - sxp[h, 7:39, :]
        curl_ref[32 * h:32 * h + 32, :] = (0.5 * diffs[h] - 0.5 * column) * share[32 * h:32 * h + 32]

    for k in range(N_PEER):
        if_other(k, lambda: back_in(k).wait_recv())
    arrived = ret_recv[...].reshape(N_TILE * CAP * NB, LANES)
    high, low = split(arrived)
    back_ref[...] = jnp.dot(gather_back, high.astype(BF16), preferred_element_type=F32) + jnp.dot(
        gather_back, low.astype(BF16), preferred_element_type=F32
    )
    for j in range(NZ):
        @pl.when(z != j)
        def _():
            own_copy(j).wait_send()

        other_direct(j).wait_send()

        @pl.when(z < j)
        def _():
            forward_up(j).wait_send()

        @pl.when((z < j) & (half == 0))
        def _():
            forward_over(j).wait_send()
    for k in range(N_PEER):
        if_other(k, lambda: back_in(k).wait_send())
    pl.when(up)(lambda: to_north.wait_send())
    pl.when(down)(lambda: to_south.wait_send())
    for copy in around:
        copy.wait_send()
    pl.when(g == N_GRP - 1)(lambda: across.wait_send())


def write_out(heat_ref, curl_ref, back_ref, heat_out, curl_out, atm_out):
    for h in range(2):
        heat_out[:, h * LANES:(h + 1) * LANES] = heat_ref[32 * h:32 * h + 32, :]
        curl_out[:, h * LANES:(h + 1) * LANES] = curl_ref[32 * h:32 * h + 32, :]
    for b in range(8):
        atm_out[:, b * LANES:(b + 1) * LANES] = back_ref[b * NB:(b + 1) * NB, :]


def per_device(atm_flux, send_block, send_count, recv_block, recv_weight, sea_temp, ocean_mask):
    hbm = pl.BlockSpec(memory_space=pl.ANY)
    vmem = pl.BlockSpec(memory_space=pltpu.VMEM)
    dma = pltpu.SemaphoreType.DMA
    heat, curl, back = pl.pallas_call(
        exchange,
        out_shape=(
            jax.ShapeDtypeStruct((64, LANES), F32),
            jax.ShapeDtypeStruct((64, LANES), F32),
            jax.ShapeDtypeStruct((32, LANES), F32),
        ),
        in_specs=[hbm] * 7,
        out_specs=(vmem, vmem, vmem),
        scratch_shapes=[
            pltpu.VMEM((NF, 1024), F32),
            pltpu.SMEM((CAP, N_TILE), jnp.int32),
            pltpu.SMEM((1, N_TILE), jnp.int32),
            pltpu.SMEM((CAP, N_TILE), jnp.int32),
            pltpu.VMEM((8, NF, LANES), F32),
            pltpu.VMEM((N_TILE, CAP, LANES, LANES), BF16),
            pltpu.VMEM((32, 256), F32),
            pltpu.VMEM((32, 256), jnp.int32),
            pltpu.VMEM((NZ, 2 * HALF, LANES), F32),
            pltpu.VMEM((NZ, HALF, LANES), F32),
            pltpu.VMEM((NZ, HALF, LANES), F32),
            pltpu.VMEM((NZ, HALF, LANES), F32),
            pltpu.VMEM((NZ, HALF, LANES), F32),
            pltpu.VMEM((512, LANES), F32),
            pltpu.VMEM((64, 8, LANES), F32),
            pltpu.VMEM((N_TILE, CAP * NB, LANES), F32),
            pltpu.VMEM((N_TILE, CAP * NB, LANES), F32),
            pltpu.VMEM((2, 48, LANES), F32),
            pltpu.VMEM((4, 8, LANES), F32),
            pltpu.VMEM((5, 8, LANES), F32),
            dma((7,)),
            dma((NZ,)),
            dma((NZ,)),
            dma((NZ,)),
            dma((NZ,)),
            dma((NZ,)),
            dma((NZ,)),
            dma((NZ,)),
            dma((NZ,)),
            dma((N_PEER,)),
            dma((N_PEER,)),
            dma((5,)),
            dma((5,)),
            pltpu.SemaphoreType.REGULAR((NZ,)),
            pltpu.SemaphoreType.REGULAR,
            pltpu.SemaphoreType.REGULAR((2,)),
        ],
        compiler_params=pltpu.CompilerParams(collective_id=0, has_side_effects=True),
        name="exchange",
    )(
        atm_flux,
        jnp.transpose(send_block[0], (1, 0)),
        send_count,
        jnp.transpose(recv_block[0], (1, 0)),
        recv_weight[0],
        sea_temp,
        ocean_mask,
    )
    return pl.pallas_call(
        write_out,
        out_shape=(
            jax.ShapeDtypeStruct((32, 256), F32),
            jax.ShapeDtypeStruct((32, 256), F32),
            jax.ShapeDtypeStruct((NB, 1024), F32),
        ),
        in_specs=[vmem, vmem, vmem],
        out_specs=(vmem, vmem, vmem),
        name="write_out",
    )(heat, curl, back)


def solution(mesh):
    placed = (
        P(None, ("grp", "tile")),
        P(("grp", "tile"), None, None),
        P(("grp", "tile"), None),
        P(("grp", "tile"), None, None),
        P(("grp", "tile"), None, None, None, None),
        P("grp", "tile"),
        P("grp", "tile"),
    )
    return jax.shard_map(
        per_device,
        mesh=mesh,
        in_specs=placed,
        out_specs=(P("grp", "tile"), P("grp", "tile"), P(None, ("grp", "tile"))),
        check_vma=False,
    )
```

time: 43.1 us -> 39.9 us (0.926); the launches traced: 42.3 us -> 39.7 us
  Pallas kernels: 41.7 us -> 39.1 us
    pallas_call x1, Pallas kernels: 40.3 us -> 37.7 us  [per_device(): pl.pallas_call(exchange, out_shape=(jax.ShapeDtypeStruct((64, LANES), F32...]
where the time goes in v2:
time: 39.9 us; the launch traced here: 39.7 us
  Pallas kernels  39.1 us (98%)
  between operations  0.64 us (2%)
    pallas_call x1, Pallas kernels, per_device(): pl.pallas_call(exchange, out_shape=(jax.ShapeDtypeStruct((64, LANES), F32...  37.7 us
    pallas_call x1, Pallas kernels, per_device(): pl.pallas_call(write_out, out_shape=(jax.ShapeDtypeStruct((32, 256), F32)...  1.41 us

profile of v2, /device:TPU:1, one launch (start us, length us, event | category | flops | bytes accessed | tf_op | source)
XLA Modules:
  0.0 39.7 jit_solution(12586957377012640557)
XLA Ops:
  0.6 37.7 %exchange.1 = (f32[64,128]{1,0:T(8,128)}, f32[64,128]{1,0:T(8,128)}, f32[32,128]{1,0:T(8,128)}) custom-call(f32[6,1024]{1,0:T(8,128)} %atm_hbm.1, s32[4,16]{1,0:T(4,128)} %bitcast.8, s32[1,16]{1,0:T(1,128)} %sc_hbm.1, s32[4,16]{1,0:T(4,128)} %bitcast.9, bf16[16,4,128,128]{3,2,1,0:T(8,128)(2,1)} %bitcast.7, f32[32,256]{1,0:T(8,128)} %temp_hbm.1, ...), custom_call_target="tpu_custom_call" | custom-call | tf_op jit(solution)/shard_map/exchange/pallas_call | solution.py:416
  38.3 1.4 %write_out.1 = (f32[32,256]{1,0:T(8,128)}, f32[32,256]{1,0:T(8,128)}, f32[4,1024]{1,0:T(4,128)}) custom-call(f32[64,128]{1,0:T(8,128)} %get-tuple-element.6.heat_ref, f32[64,128]{1,0:T(8,128)} %get-tuple-element.7.curl_ref, f32[32,128]{1,0:T(8,128)} %get-tuple-element.8.back_ref), custom_call_target="tpu_custom_call" | custom-call | tf_op jit(solution)/shard_map/write_out/pallas_call | solution.py:474

commit v3 on v2

--- a/solution.py
+++ b/solution.py
@@ -59,7 +59,7 @@
     for load in loads[:4]:
         load.start()
     up, down = g < N_GRP - 1, g > 0
-    last8, first8 = lax.rem(g, 8) == 7, lax.rem(g, 8) == 0
+    last8, first8 = (lax.rem(g, 8) == 7) | (g == 0), (lax.rem(g, 8) == 0) | (g == 1)
     barrier = pltpu.get_barrier_semaphore()
     for j in range(NZ - 1, 0, -1):
         @pl.when(z < j)
@@ -76,7 +76,8 @@
 
     for load in loads[4:]:
         load.start()
-    is_last8, not_first8 = lax.rem(g, 8) // 7, jnp.minimum(lax.rem(g, 8), 1)
+    is_last8 = lax.rem(g, 8) // 7 + shift
+    not_first8 = jnp.minimum(lax.rem(g, 8), 1) * jnp.minimum(jnp.maximum(g, 1) - 1, 1)
     below = jnp.minimum(g, 1) * not_first8
     above = is_last8 * jnp.minimum(N_GRP - 1 - g, 1)
     earlier = z + half + below + above
@@ -164,29 +165,45 @@
         pl.semaphore_wait(partner_in, 1)
 
     other_direct(z).start()
-    for j in range(1, NZ):
-        @pl.when(z < j)
-        def _():
-            other_up(j).start()
-    for j in range(1, NZ):
-        @pl.when(z < j)
-        def _():
-            pl.semaphore_wait(column_in.at[j], 1)
-            own_copy(j).start()
-    def pass_on_up():
+
+    def push_up(j):
+        pl.semaphore_wait(column_in.at[j], 1)
+        own_copy(j).start()
+
+    def pass_up_to(j):
+        other_up(j).wait_recv()
+        forward_up(j).start()
+
+    def pass_over_from(j):
+        @pl.when(half == 0)
+        def _():
+            over_in(j).wait_recv()
+            forward_over(j).start()
+
+    @pl.when(z < NZ // 2)
+    def _():
+        for j in range(1, NZ):
+            pl.when(z < j)(lambda: other_up(j).start())
         for j in range(1, NZ):
             @pl.when(z < j)
             def _():
-                other_up(j).wait_recv()
-                forward_up(j).start()
-
-    pl.when(z < NZ // 2)(pass_on_up)
-    for j in range(1, NZ):
-        @pl.when((z < j) & (half == 0))
-        def _():
-            over_in(j).wait_recv()
-            forward_over(j).start()
-    pl.when(z >= NZ // 2)(pass_on_up)
+                push_up(j)
+                pass_up_to(j)
+
+            pl.when(z < j - 1)(lambda: pass_over_from(j - 1))
+        pass_over_from(NZ - 1)
+
+    @pl.when(z >= NZ // 2)
+    def _():
+        levels = range(NZ // 2 + 1, NZ)
+        for j in reversed(levels):
+            pl.when(z < j)(lambda: other_up(j).start())
+        for j in levels:
+            pl.when(z < j)(lambda: push_up(j))
+        for j in levels:
+            pl.when(z < j)(lambda: pass_over_from(j))
+        for j in reversed(levels):
+            pl.when(z < j)(lambda: pass_up_to(j))
 
     lane = lax.broadcasted_iota(jnp.int32, (8, LANES), 1)
     dest = jnp.full((8, LANES), -1, jnp.int32)
@@ -416,9 +433,9 @@
     heat, curl, back = pl.pallas_call(
         exchange,
         out_shape=(
-            jax.ShapeDtypeStruct((64, LANES), F32),
-            jax.ShapeDtypeStruct((64, LANES), F32),
-            jax.ShapeDtypeStruct((32, LANES), F32),
+            pltpu.VMEM((64, LANES), F32),
+            pltpu.VMEM((64, LANES), F32),
+            pltpu.VMEM((32, LANES), F32),
         ),
         in_specs=[hbm] * 7,
         out_specs=(vmem, vmem, vmem),
@@ -481,7 +498,7 @@
         in_specs=[vmem, vmem, vmem],
         out_specs=(vmem, vmem, vmem),
         name="write_out",
-    )(heat, curl, back)
+    )(*[pltpu.with_memory_space_constraint(x, pltpu.VMEM) for x in (heat, curl, back)])
 
 
 def solution(mesh):

time: 39.9 us -> 38.4 us (0.962)
  the two profiles are of different devices: /device:TPU:1 before, /device:TPU:38 now
where the time goes in v3:
time: 38.4 us; the launch traced here: 38.2 us
  Pallas kernels  37.6 us (98%)
  between operations  0.64 us (2%)
    pallas_call x1, Pallas kernels, per_device(): pl.pallas_call(exchange, out_shape=(pltpu.VMEM((64, LANES), F32), pltpu.V...  36.9 us

profile of v3, /device:TPU:38, one launch (start us, length us, event | category | flops | bytes accessed | tf_op | source)
XLA Modules:
  0.0 38.2 jit_solution(8608377892414225844)
XLA Ops:
  0.6 36.9 %exchange.1 = (f32[64,128]{1,0:T(8,128)S(1)}, f32[64,128]{1,0:T(8,128)S(1)}, f32[32,128]{1,0:T(8,128)S(1)}) custom-call(f32[6,1024]{1,0:T(8,128)} %atm_hbm.1, s32[4,16]{1,0:T(4,128)} %bitcast.8, s32[1,16]{1,0:T(1,128)} %sc_hbm.1, s32[4,16]{1,0:T(4,128)} %bitcast.9, bf16[16,4,128,128]{3,2,1,0:T(8,128)(2,1)} %bitcast.7, f32[32,256]{1,0:T(8,128)} %temp_hbm.1, ...), custom_call_target="tpu_custom_call" | custom-call | tf_op jit(solution)/shard_map/exchange/pallas_call | solution.py:433
  37.6 0.6 %write_out.1 = (f32[32,256]{1,0:T(8,128)}, f32[32,256]{1,0:T(8,128)}, f32[4,1024]{1,0:T(4,128)}) custom-call(f32[64,128]{1,0:T(8,128)S(1)} %get-tuple-element.6.heat_ref, f32[64,128]{1,0:T(8,128)S(1)} %get-tuple-element.7.curl_ref, f32[32,128]{1,0:T(8,128)S(1)} %get-tuple-element.8.back_ref), custom_call_target="tpu_custom_call" | custom-call | tf_op jit(solution)/shard_map/write_out/pallas_call | solution.py:491

commit v4 on v3

--- a/solution.py
+++ b/solution.py
@@ -321,7 +321,7 @@
         else:
             act()
 
-    order = [k for j in range(NZ) for k in (NZ + j, j)]
+    order = [NZ + j for j in range(NZ)] + list(range(NZ))
     for i, k in enumerate(order):
         for c in range(CAP):
             high, low = split(surf[rb_ref[c, peer(k)]])
@@ -349,7 +349,6 @@
         pick32 = jnp.concatenate([pick] * 4, axis=0)
         hit = (row32 // NB == pick32) & (lax.rem(row32, NB) == lax.rem(lane32, NB))
         picks.append(jnp.where(hit, 1.0, 0.0).astype(BF16))
-    gather_back = jnp.concatenate(picks, axis=1)
 
     pl.when(up)(lambda: to_south.wait_recv())
     pl.when(down)(lambda: to_north.wait_recv())
@@ -388,13 +387,6 @@
         column = sxp[h, 9:41, :] - sxp[h, 7:39, :]
         curl_ref[32 * h:32 * h + 32, :] = (0.5 * diffs[h] - 0.5 * column) * share[32 * h:32 * h + 32]
 
-    for k in range(N_PEER):
-        if_other(k, lambda: back_in(k).wait_recv())
-    arrived = ret_recv[...].reshape(N_TILE * CAP * NB, LANES)
-    high, low = split(arrived)
-    back_ref[...] = jnp.dot(gather_back, high.astype(BF16), preferred_element_type=F32) + jnp.dot(
-        gather_back, low.astype(BF16), preferred_element_type=F32
-    )
     for j in range(NZ):
         @pl.when(z != j)
         def _():
@@ -416,6 +408,14 @@
     for copy in around:
         copy.wait_send()
     pl.when(g == N_GRP - 1)(lambda: across.wait_send())
+    total = jnp.zeros((32, LANES), F32)
+    for part in range(2):
+        for k in range(8 * part, 8 * part + 8):
+            if_other(k, lambda: back_in(k).wait_recv())
+        high, low = split(ret_recv[8 * part:8 * part + 8].reshape(8 * CAP * NB, LANES))
+        total += jnp.dot(picks[part], high.astype(BF16), preferred_element_type=F32)
+        total += jnp.dot(picks[part], low.astype(BF16), preferred_element_type=F32)
+    back_ref[...] = total
 
 
 def write_out(heat_ref, curl_ref, back_ref, heat_out, curl_out, atm_out):

time: 38.4 us -> 38.4 us (level)
  the two profiles are of different devices: /device:TPU:38 before, /device:TPU:36 now
where the time goes in v4:
time: 38.4 us; the launch traced here: 38.3 us
  Pallas kernels  37.7 us (98%)
  between operations  0.64 us (2%)
    pallas_call x1, Pallas kernels, per_device(): pl.pallas_call(exchange, out_shape=(pltpu.VMEM((64, LANES), F32), pltpu.V...  37 us

profile of v4, /device:TPU:36, one launch (start us, length us, event | category | flops | bytes accessed | tf_op | source)
XLA Modules:
  0.0 38.3 jit_solution(16371104485174495482)
XLA Ops:
  0.6 37.0 %exchange.1 = (f32[64,128]{1,0:T(8,128)S(1)}, f32[64,128]{1,0:T(8,128)S(1)}, f32[32,128]{1,0:T(8,128)S(1)}) custom-call(f32[6,1024]{1,0:T(8,128)} %atm_hbm.1, s32[4,16]{1,0:T(4,128)} %bitcast.8, s32[1,16]{1,0:T(1,128)} %sc_hbm.1, s32[4,16]{1,0:T(4,128)} %bitcast.9, bf16[16,4,128,128]{3,2,1,0:T(8,128)(2,1)} %bitcast.7, f32[32,256]{1,0:T(8,128)} %temp_hbm.1, ...), custom_call_target="tpu_custom_call" | custom-call | tf_op jit(solution)/shard_map/exchange/pallas_call | solution.py:433
  37.7 0.6 %write_out.1 = (f32[32,256]{1,0:T(8,128)}, f32[32,256]{1,0:T(8,128)}, f32[4,1024]{1,0:T(4,128)}) custom-call(f32[64,128]{1,0:T(8,128)S(1)} %get-tuple-element.6.heat_ref, f32[64,128]{1,0:T(8,128)S(1)} %get-tuple-element.7.curl_ref, f32[32,128]{1,0:T(8,128)S(1)} %get-tuple-element.8.back_ref), custom_call_target="tpu_custom_call" | custom-call | tf_op jit(solution)/shard_map/write_out/pallas_call | solution.py:491
